TPU v7x, 512 devices: a whole 4x4x16 slice. The times are simulated.
512 devices in a mesh: dp: 8 (over y, core), seq: 16 (over z), head: 4 (over x).
Axes of the slice: x: 4, y: 4, z: 16, core: 2. Of those that a mesh axis runs over, the one named last changes fastest.
Arguments:
- queries: bfloat16 [8, 4096, 3072], P('dp', 'seq', 'head'), may hold values from -60 to 60
- key_rows: bfloat16 [8, 4096, 3072], P('dp', 'seq', 'head'), may hold values from -4.5 to 4.5
- value_rows: bfloat16 [8, 4096, 3072], P('dp', 'seq', 'head'), may hold values from -4 to 4
- out_grad: bfloat16 [8, 4096, 3072], P('dp', 'seq', 'head'), may hold values from -9.5 to 9.5
- tile_image: int32 [8, 32], P('dp'), may hold values from 0 to 7, never falling along the last dimension, each value on 1 to 6 neighbouring positions
Outputs:
- attn_out: bfloat16 [8, 4096, 3072], P('dp', 'seq', 'head')
- query_grad: bfloat16 [8, 4096, 3072], P('dp', 'seq', 'head')
- key_grad: bfloat16 [8, 4096, 3072], P('dp', 'seq', 'head')
- value_grad: bfloat16 [8, 4096, 3072], P('dp', 'seq', 'head')
- grad_rms: float32 [], replicated
Inputs may be any that keep to these rules, and one draw needn't show every extreme that they name: `tile_image`: image numbers never fall along a sequence; every image covers 1 to 6 whole tiles of 128 patches, and in each sequence one image covers exactly 6 tiles.
All inputs are finite; a program needn't handle non-finite values.
Results may differ from a plain program's by a relative error of at most 0.0073.
Values may be sent and summed in bfloat16 or wider, within the bound.
A program may use at most 64 MiB of HBM per device.

v0:
```python
import functools

import jax
import jax.numpy as jnp
from jax import lax
from jax.experimental import pallas as pl
from jax.experimental.pallas import tpu as pltpu
from jax.sharding import PartitionSpec as P

HEAD_DIM = 128
TILE = 128
OWN = 2
WINDOW = 8
ROWS = WINDOW * TILE
BLOCK = 256
MESH = pl.DeviceIdType.MESH


def rows_of(tile, count=1):
    return pl.ds(tile * TILE, count * TILE)


def kernel(
    tiles_ref,
    q_hbm,
    k_hbm,
    v_hbm,
    g_hbm,
    o_ref,
    dq_ref,
    dk_ref,
    dv_ref,
    rms_ref,
    win,
    outs,
    stage,
    got_a,
    got_b,
    bias,
    dk_acc,
    dv_acc,
    squares,
    line_sums,
    plane_sums,
    load_sem,
    own_send,
    own_recv,
    a_send,
    a_recv,
    b_send,
    b_recv,
    line_send,
    line_recv,
    plane_send,
    plane_recv,
    *,
    heads,
    line,
    dps,
    heads_axis,
    total,
):
    me = lax.axis_index("seq")
    my_dp = lax.axis_index("dp")
    my_head = lax.axis_index("head")
    scale = HEAD_DIM ** (-0.5)
    has_left = me > 0
    has_right = me < line - 1
    left = jnp.maximum(me - 1, 0)
    right = jnp.minimum(me + 1, line - 1)
    tile_count = OWN * line

    def load(source, slot, head):
        return pltpu.make_async_copy(
            source.at[0, :, pl.ds(head * HEAD_DIM, HEAD_DIM)],
            win.at[head, slot, rows_of(3, 2), :],
            load_sem.at[head, slot],
        )

    def own_copy(head, way):
        return pltpu.make_async_remote_copy(
            src_ref=win.at[head, :, rows_of(3, 2), :],
            dst_ref=win.at[head, :, rows_of(1 if way == 0 else 5, 2), :],
            send_sem=own_send.at[way, head],
            recv_sem=own_recv.at[way, head],
            device_id={"seq": right if way == 0 else left},
            device_id_type=MESH,
        )

    def a_copy(head, way):
        return pltpu.make_async_remote_copy(
            src_ref=stage.at[way, head],
            dst_ref=got_a.at[way, head],
            send_sem=a_send.at[way, head],
            recv_sem=a_recv.at[way, head],
            device_id={"seq": right if way == 0 else left},
            device_id_type=MESH,
        )

    def b_copy(head, way):
        return pltpu.make_async_remote_copy(
            src_ref=outs.at[head, :, rows_of(6 if way == 0 else 1), :],
            dst_ref=got_b.at[way, head],
            send_sem=b_send.at[way, head],
            recv_sem=b_recv.at[way, head],
            device_id={"seq": right if way == 0 else left},
            device_id_type=MESH,
        )

    def each_start(copy, head):
        @pl.when(has_right)
        def _():
            copy(head, 0).start()

        @pl.when(has_left)
        def _():
            copy(head, 1).start()

    def each_wait_recv(copy, head):
        @pl.when(has_left)
        def _():
            copy(head, 0).wait_recv()

        @pl.when(has_right)
        def _():
            copy(head, 1).wait_recv()

    def each_wait_send(copy, head):
        @pl.when(has_right)
        def _():
            copy(head, 0).wait_send()

        @pl.when(has_left)
        def _():
            copy(head, 1).wait_send()

    for head in range(heads):
        for slot, source in enumerate((q_hbm, k_hbm, v_hbm, g_hbm)):
            load(source, slot, head).start()

    @pl.when(jnp.logical_not(has_left))
    def _():
        win[:, :, rows_of(0, 3), :] = jnp.zeros((heads, 4, 3 * TILE, HEAD_DIM), jnp.bfloat16)

    @pl.when(jnp.logical_not(has_right))
    def _():
        win[:, :, rows_of(5, 3), :] = jnp.zeros((heads, 4, 3 * TILE, HEAD_DIM), jnp.bfloat16)

    barrier = pltpu.get_barrier_semaphore()

    def greet_line(step, carry):
        pl.semaphore_signal(
            barrier,
            inc=1,
            device_id={"seq": lax.rem(me + step, line)},
            device_id_type=MESH,
        )
        return carry

    def plane_peer(step):
        place = lax.rem(my_dp * heads_axis + my_head + step, dps * heads_axis)
        return place // heads_axis, lax.rem(place, heads_axis)

    def greet_plane(step, carry):
        peer_dp, peer_head = plane_peer(step)
        pl.semaphore_signal(
            barrier,
            inc=1,
            device_id={"dp": peer_dp, "head": peer_head},
            device_id_type=MESH,
        )
        return carry

    lax.fori_loop(1, line, greet_line, 0)
    lax.fori_loop(1, dps * heads_axis, greet_plane, 0)

    images = []
    for place in range(WINDOW):
        tile = OWN * me - 3 + place
        image = tiles_ref[0, jnp.clip(tile, 0, tile_count - 1)]
        image = jnp.where(tile < 0, -1, image)
        images.append(jnp.where(tile >= tile_count, -2, image))
    over_left = images[0] == images[5]
    over_right = images[2] == images[7]
    names = list(images)
    names[0] = jnp.where(over_left, images[0], -3)
    names[7] = jnp.where(over_right, images[7], -4)
    for row in range(WINDOW):
        for column in range(WINDOW):
            level = jnp.where(names[row] == names[column], 0.0, -jnp.inf).astype(jnp.float32)
            bias[row : row + 1, column * TILE : (column + 1) * TILE] = jnp.full(
                (1, TILE), level, jnp.float32
            )
    not_left = jnp.logical_not(over_left)
    not_right = jnp.logical_not(over_right)
    from_left = [jnp.logical_and(images[w] == images[0], not_left) for w in (3, 4)]
    from_right = [jnp.logical_and(images[w] == images[7], not_right) for w in (3, 4)]
    mine = {}
    for w in (1, 2):
        mine[w] = jnp.logical_and(images[w] == images[5], not_left)
    for w in (5, 6):
        mine[w] = jnp.logical_and(images[w] == images[2], not_right)
    for index, w in enumerate((3, 4)):
        mine[w] = jnp.logical_not(jnp.logical_or(from_left[index], from_right[index]))
    squares[...] = jnp.zeros((8, 128), jnp.float32)

    pl.semaphore_wait(barrier, line - 1 + dps * heads_axis - 1)

    def send_own(head):
        for slot, source in enumerate((q_hbm, k_hbm, v_hbm, g_hbm)):
            load(source, slot, head).wait()
        each_start(own_copy, head)

    for head in range(min(2, heads)):
        send_own(head)

    def add_squares(value, flag):
        wide = value.astype(jnp.float32)
        wide = jnp.sum((wide * wide).reshape(TILE // 8, 8, HEAD_DIM), axis=0)
        squares[...] += jnp.where(flag, wide, 0.0)

    def compute(head):
        dk_acc[...] = jnp.zeros((HEAD_DIM, ROWS), jnp.float32)
        dv_acc[...] = jnp.zeros((HEAD_DIM, ROWS), jnp.float32)
        lanes = (((1,), (1,)), ((), ()))
        rows = (((0,), (0,)), ((), ()))
        wide = jnp.float32

        def block(index, carry):
            here = pl.ds(pl.multiple_of(index * BLOCK, BLOCK), BLOCK)
            query = win[head, 0, here, :]
            grad = win[head, 3, here, :]
            keys = win[head, 1]
            values = win[head, 2]
            scores = lax.dot_general(query, keys, lanes, preferred_element_type=wide) * scale
            pieces = []
            for half in range(BLOCK // TILE):
                row = bias[pl.ds(index * (BLOCK // TILE) + half, 1), :]
                pieces.append(scores[half * TILE : (half + 1) * TILE] + row)
            scores = jnp.concatenate(pieces, axis=0)
            raised = jnp.exp(scores - jnp.max(scores, axis=1, keepdims=True))
            weights = raised * (1.0 / jnp.sum(raised, axis=1, keepdims=True))
            weights = weights.astype(jnp.bfloat16)
            out = jnp.dot(weights, values, preferred_element_type=wide).astype(jnp.bfloat16)
            outs[head, 0, here, :] = out
            delta = jnp.sum(grad.astype(wide) * out.astype(wide), axis=1, keepdims=True)
            dweights = lax.dot_general(grad, values, lanes, preferred_element_type=wide)
            dscores = (weights.astype(wide) * (dweights - delta)).astype(jnp.bfloat16)
            dquery = jnp.dot(dscores, keys, preferred_element_type=wide) * scale
            outs[head, 1, here, :] = dquery.astype(jnp.bfloat16)
            dk_acc[...] += lax.dot_general(query, dscores, rows, preferred_element_type=wide)
            dv_acc[...] += lax.dot_general(grad, weights, rows, preferred_element_type=wide)
            return carry

        lax.fori_loop(0, ROWS // BLOCK, block, 0)
        for w in range(1, WINDOW - 1):
            dk = jnp.transpose(dk_acc[:, w * TILE : (w + 1) * TILE] * scale).astype(jnp.bfloat16)
            dv = jnp.transpose(dv_acc[:, w * TILE : (w + 1) * TILE]).astype(jnp.bfloat16)
            outs[head, 2, rows_of(w), :] = dk
            outs[head, 3, rows_of(w), :] = dv
            add_squares(outs[head, 1, rows_of(w), :], mine[w])
            add_squares(dk, mine[w])
            add_squares(dv, mine[w])

    out_refs = (o_ref, dq_ref, dk_ref, dv_ref)

    def assemble(head):
        column = pl.ds(pl.multiple_of(head * HEAD_DIM, HEAD_DIM), HEAD_DIM)
        each_wait_recv(b_copy, head)
        for slot, out_ref in enumerate(out_refs):
            first = outs[head, slot, rows_of(3), :]
            first = jnp.where(from_left[0], got_a[0, head + 1, slot], first)
            first = jnp.where(from_right[0], got_b[1, head, slot], first)
            out_ref[0, rows_of(0), column] = first
            second = outs[head, slot, rows_of(4), :]
            second = jnp.where(from_left[1], got_b[0, head, slot], second)
            second = jnp.where(from_right[1], got_a[1, head + 1, slot], second)
            out_ref[0, rows_of(1), column] = second

    def fill_stage(head, previous):
        for way, place, switch, back in ((0, 2, over_right, 5), (1, 5, over_left, 2)):
            for slot in range(4):
                passed = win[head, slot, rows_of(place), :]
                if previous is None:
                    other = jnp.zeros((TILE, HEAD_DIM), jnp.bfloat16)
                else:
                    other = outs[previous, slot, rows_of(back), :]
                stage[way, head, slot] = jnp.where(switch, passed, other)

    def step(head, carry):
        each_wait_recv(own_copy, head)

        @pl.when(head == 0)
        def _():
            fill_stage(head, None)

        @pl.when(head > 0)
        def _():
            fill_stage(head, head - 1)

        each_start(a_copy, head)

        @pl.when(head + 2 < heads)
        def _():
            send_own(head + 2)

        @pl.when(head > 0)
        def _():
            each_start(b_copy, head - 1)

        each_wait_recv(a_copy, head)
        blank = jnp.zeros((TILE, HEAD_DIM), jnp.bfloat16)
        for slot in range(4):
            win[head, slot, rows_of(0), :] = jnp.where(over_left, got_a[0, head, slot], blank)
            win[head, slot, rows_of(7), :] = jnp.where(over_right, got_a[1, head, slot], blank)
        compute(head)

        @pl.when(head >= 2)
        def _():
            assemble(head - 2)

        return carry

    lax.fori_loop(0, heads, step, 0)

    line_sums[pl.ds(me, 1)] = squares[...][None]

    def line_copy(step):
        return pltpu.make_async_remote_copy(
            src_ref=squares,
            dst_ref=line_sums.at[me],
            send_sem=line_send.at[step],
            recv_sem=line_recv.at[me],
            device_id={"seq": lax.rem(me + step, line)},
            device_id_type=MESH,
        )

    def line_arrival(step):
        peer = lax.rem(me + step, line)
        return pltpu.make_async_remote_copy(
            src_ref=squares,
            dst_ref=line_sums.at[peer],
            send_sem=line_send.at[step],
            recv_sem=line_recv.at[peer],
            device_id={"seq": peer},
            device_id_type=MESH,
        )

    def over(count, action):
        def body(step, carry):
            action(step)
            return carry

        lax.fori_loop(1, count, body, 0)

    over(line, lambda step: line_copy(step).start())

    fill_stage_last = ((0, 5), (1, 2))
    for way, back in fill_stage_last:
        for slot in range(4):
            stage[way, heads, slot] = outs[heads - 1, slot, rows_of(back), :]
    each_start(a_copy, heads)
    each_start(b_copy, heads - 1)

    if heads >= 2:
        assemble(heads - 2)

    over(line, lambda step: line_arrival(step).wait_recv())
    place = my_dp * heads_axis + my_head
    line_total = jnp.sum(line_sums[...], axis=0)
    squares_line = plane_sums.at[place]
    squares_line[...] = line_total

    def plane_copy(step, slot):
        peer_dp, peer_head = plane_peer(step)
        return pltpu.make_async_remote_copy(
            src_ref=plane_sums.at[place],
            dst_ref=plane_sums.at[slot],
            send_sem=plane_send.at[step],
            recv_sem=plane_recv.at[slot],
            device_id={"dp": peer_dp, "head": peer_head},
            device_id_type=MESH,
        )

    plane = dps * heads_axis
    over(plane, lambda step: plane_copy(step, place).start())

    each_wait_recv(a_copy, heads)
    assemble(heads - 1)

    over(plane, lambda step: plane_copy(step, lax.rem(place + step, plane)).wait_recv())
    everything = jnp.sum(plane_sums[...], axis=0)
    everything = jnp.sum(everything, axis=1, keepdims=True)
    everything = jnp.sum(everything, axis=0, keepdims=True)
    rms_ref[0] = jnp.sqrt(everything * (1.0 / total))[0, 0]

    def finish(head, carry):
        each_wait_send(own_copy, head)
        each_wait_send(a_copy, head)
        each_wait_send(b_copy, head)
        return carry

    lax.fori_loop(0, heads, finish, 0)
    each_wait_send(a_copy, heads)
    over(line, lambda step: line_copy(step).wait_send())
    over(plane, lambda step: plane_copy(step, place).wait_send())


def solution(mesh):
    line, dps, heads_axis = mesh.shape["seq"], mesh.shape["dp"], mesh.shape["head"]

    def shards(queries, key_rows, value_rows, out_grad, tile_image):
        _, rows, features = queries.shape
        heads = features // HEAD_DIM
        total = 3.0 * rows * features * line * dps * heads_axis
        result = jax.ShapeDtypeStruct((1, rows, features), jnp.bfloat16)
        tile = (4, TILE, HEAD_DIM)
        bf16, f32 = jnp.bfloat16, jnp.float32
        dma = pltpu.SemaphoreType.DMA
        vmem = pl.BlockSpec(memory_space=pltpu.VMEM)
        smem = pl.BlockSpec(memory_space=pltpu.SMEM)
        hbm = pl.BlockSpec(memory_space=pl.ANY)
        outputs = pl.pallas_call(
            functools.partial(
                kernel, heads=heads, line=line, dps=dps, heads_axis=heads_axis, total=total
            ),
            out_shape=(result, result, result, result, jax.ShapeDtypeStruct((1,), f32)),
            in_specs=[smem, hbm, hbm, hbm, hbm],
            out_specs=(vmem, vmem, vmem, vmem, smem),
            scratch_shapes=[
                pltpu.VMEM((heads, 4, ROWS, HEAD_DIM), bf16),
                pltpu.VMEM((heads, 4, ROWS, HEAD_DIM), bf16),
                pltpu.VMEM((2, heads + 1) + tile, bf16),
                pltpu.VMEM((2, heads + 1) + tile, bf16),
                pltpu.VMEM((2, heads) + tile, bf16),
                pltpu.VMEM((WINDOW, ROWS), f32),
                pltpu.VMEM((HEAD_DIM, ROWS), f32),
                pltpu.VMEM((HEAD_DIM, ROWS), f32),
                pltpu.VMEM((8, 128), f32),
                pltpu.VMEM((line, 8, 128), f32),
                pltpu.VMEM((dps * heads_axis, 8, 128), f32),
                dma((heads, 4)),
                dma((2, heads)),
                dma((2, heads)),
                dma((2, heads + 1)),
                dma((2, heads + 1)),
                dma((2, heads)),
                dma((2, heads)),
                dma((line,)),
                dma((line,)),
                dma((dps * heads_axis,)),
                dma((dps * heads_axis,)),
            ],
            compiler_params=pltpu.CompilerParams(
                collective_id=0, has_side_effects=True, vmem_limit_bytes=48 * 1024 * 1024
            ),
        )(tile_image, queries, key_rows, value_rows, out_grad)
        return outputs[:4] + (outputs[4].reshape(()),)

    wide = P("dp", "seq", "head")
    return jax.shard_map(
        shards,
        mesh=mesh,
        in_specs=(wide, wide, wide, wide, P("dp", None)),
        out_specs=(wide, wide, wide, wide, P()),
        check_vma=False,
    )
```

profile of v0, /device:TPU:1, one launch (start us, length us, event | category | flops | bytes accessed | tf_op | source)
XLA Modules:
  0.0 120.2 jit_solution(1916425954983476654)
XLA Ops:
  0.6 0.0 copy-start
  0.6 1.0 copy-done
  1.6 0.0 copy-start.1
  1.6 1.0 copy-done.1
  2.6 0.0 copy-start.2
  2.6 1.0 copy-done.2
  3.6 0.0 copy-start.3
  3.6 1.0 copy-done.3
  4.6 0.0 copy-start.4
  4.6 0.7 copy-done.4
  5.3 110.3 %shard_map.92 = (bf16[1,256,768]{2,1,0:T(8,128)(2,1)S(1)}, bf16[1,256,768]{2,1,0:T(8,128)(2,1)S(1)}, bf16[1,256,768]{2,1,0:T(8,128)(2,1)S(1)}, bf16[1,256,768]{2,1,0:T(8,128)(2,1)S(1)}, f32[1]{0:T(128)}) custom-call(s32[1,32]{1,0:T(1,128)S(1)} %copy-done.4, bf16[1,256,768]{2,1,0:T(8,128)(2,1)S(1)} %copy-done, bf16[1,256,768]{2,1,0:T(8,128)(2,1)S(1)} %copy-done.1, ...), custom_call_target="tpu_custom_call" | custom-call | tf_op jit(solution)/shard_map/pallas_call | solution.py:423
  115.6 0.7 copy.15
  116.3 0.7 copy.16
  117.1 0.7 copy.17
  117.8 0.7 copy.18
Async XLA Ops:
  0.6 1.0 copy-start
  1.6 1.0 copy-start.1
  2.6 1.0 copy-start.2
  3.6 1.0 copy-start.3
  4.6 0.7 copy-start.4
where the time goes:
time: 121 us; the launch traced here: 120 us
  Pallas kernels  110 us (91%)
  local copies, waits for them, and re-layouts  7.61 us (6%)
  between operations  2.34 us (2%)
    pallas_call x1, Pallas kernels, shards(): pl.pallas_call(functools.partial(kernel, heads=heads, line=line, dps=dps,...  110 us
    unnamed x14, local copies, waits for them, and re-layouts  7.61 us

commit v1 on v0

v1 whole, which is shorter than its diff:
```python
import functools

import jax
import jax.numpy as jnp
from jax import lax
from jax.experimental import pallas as pl
from jax.experimental.pallas import tpu as pltpu
from jax.sharding import PartitionSpec as P

HEAD_DIM = 128
TILE = 128
OWN = 2
WINDOW = 8
ROWS = WINDOW * TILE
BLOCK = 256
LAG = 3
MESH = pl.DeviceIdType.MESH


def rows_of(tile, count=1):
    return pl.ds(tile * TILE, count * TILE)


def kernel(
    tiles_ref,
    q_hbm,
    k_hbm,
    v_hbm,
    g_hbm,
    o_ref,
    dq_ref,
    dk_ref,
    dv_ref,
    rms_ref,
    win,
    outs,
    stage,
    got_m,
    got_t,
    bias,
    dk_acc,
    dv_acc,
    squares,
    own_sum,
    line_sums,
    plane_sums,
    load_sem,
    m_send,
    m_recv,
    t_send,
    t_recv,
    token,
    line_send,
    line_recv,
    plane_send,
    plane_recv,
    *,
    heads,
    line,
    dps,
    heads_axis,
    total,
):
    me = lax.axis_index("seq")
    my_dp = lax.axis_index("dp")
    my_head = lax.axis_index("head")
    scale = HEAD_DIM ** (-0.5)
    has_left = me > 0
    has_right = me < line - 1
    left = jnp.maximum(me - 1, 0)
    right = jnp.minimum(me + 1, line - 1)
    tile_count = OWN * line

    def load(source, slot, head):
        return pltpu.make_async_copy(
            source.at[0, :, pl.ds(head * HEAD_DIM, HEAD_DIM)],
            win.at[head, slot, rows_of(3, 2), :],
            load_sem.at[head, slot],
        )

    def sent(source, target, send, recv, way):
        return pltpu.make_async_remote_copy(
            src_ref=source,
            dst_ref=target,
            send_sem=send,
            recv_sem=recv,
            device_id={"seq": right if way == 0 else left},
            device_id_type=MESH,
        )

    def m_copy(turn, way, source):
        return sent(
            source, got_m.at[way, turn], m_send.at[way, turn], m_recv.at[way, turn], way
        )

    def m_inputs(turn, way):
        return m_copy(turn, way, win.at[turn, :, rows_of(3, 2), :])

    def m_either(turn, way):
        return m_copy(turn, way, stage.at[way, turn - LAG])

    def m_results(turn, way):
        return m_copy(turn, way, outs.at[turn - LAG, :, rows_of(5 if way == 0 else 1, 2), :])

    def t_copy(head, way):
        return sent(
            got_m.at[way, head, :, rows_of(1 if way == 0 else 0), :],
            got_t.at[way, head],
            t_send.at[way, head],
            t_recv.at[way, head],
            way,
        )

    inner = jnp.logical_and(has_left, has_right)

    def m_start(copy, turn):
        @pl.when(has_right)
        def _():
            copy(turn, 0).start()

        @pl.when(has_left)
        def _():
            copy(turn, 1).start()

    def m_wait_recv(turn):
        @pl.when(has_left)
        def _():
            m_copy(turn, 0, got_m.at[0, turn]).wait_recv()

        @pl.when(has_right)
        def _():
            m_copy(turn, 1, got_m.at[1, turn]).wait_recv()

    def m_wait_send(copy, turn):
        @pl.when(has_right)
        def _():
            copy(turn, 0).wait_send()

        @pl.when(has_left)
        def _():
            copy(turn, 1).wait_send()

    def t_start(head):
        @pl.when(inner)
        def _():
            t_copy(head, 0).start()
            t_copy(head, 1).start()

    def t_wait_recv(head):
        @pl.when(me > 1)
        def _():
            t_copy(head, 0).wait_recv()

        @pl.when(me < line - 2)
        def _():
            t_copy(head, 1).wait_recv()

    def t_wait_send(head):
        @pl.when(inner)
        def _():
            t_copy(head, 0).wait_send()
            t_copy(head, 1).wait_send()

    for head in range(heads):
        for slot, source in enumerate((q_hbm, k_hbm, v_hbm, g_hbm)):
            load(source, slot, head).start()

    barrier = pltpu.get_barrier_semaphore()

    near = []

    def ring(axis, place, count, stride):
        length = count // stride
        hop = place // stride
        if length == 2:
            near.append(({axis: lax.rem(place + stride, count)}, len(near)))
        elif length > 2:
            first = len(near)
            near.append(({axis: lax.rem(hop + 1, length) * stride + lax.rem(place, stride)}, first + 1))
            near.append(
                ({axis: lax.rem(hop + length - 1, length) * stride + lax.rem(place, stride)}, first)
            )

    ring("seq", me, line, 1)
    ring("head", my_head, heads_axis, 1)
    cores = 2 if dps % 2 == 0 else 1
    ring("dp", my_dp, dps, cores)
    if cores == 2:
        near.append(({"dp": my_dp + 1 - 2 * lax.rem(my_dp, 2)}, len(near)))

    def give_tokens():
        for peer, heard in near:
            pl.semaphore_signal(token.at[heard], inc=1, device_id=peer, device_id_type=MESH)

    def take_tokens():
        for index in range(len(near)):
            pl.semaphore_wait(token.at[index], 1)

    def plane_peer(step):
        place = lax.rem(my_dp * heads_axis + my_head + step, dps * heads_axis)
        return place // heads_axis, lax.rem(place, heads_axis)

    for peer, _ in near:
        pl.semaphore_signal(barrier, inc=1, device_id=peer, device_id_type=MESH)

    images = []
    for place in range(WINDOW):
        tile = OWN * me - 3 + place
        image = tiles_ref[0, jnp.clip(tile, 0, tile_count - 1)]
        image = jnp.where(tile < 0, -1, image)
        images.append(jnp.where(tile >= tile_count, -2, image))

    def border(tiles):
        crossing = tiles[2] == tiles[3]
        a2, a3 = tiles[1] == tiles[2], tiles[0] == tiles[2]
        b2, b3 = tiles[4] == tiles[3], tiles[5] == tiles[3]
        both = jnp.logical_and(crossing, jnp.logical_and(a3, b3))
        fewer_right = jnp.logical_or(
            jnp.logical_and(a3, jnp.logical_not(b3)), jnp.logical_and(a2, jnp.logical_not(b2))
        )
        at_left = jnp.logical_and(crossing, fewer_right)
        at_right = jnp.logical_not(jnp.logical_or(at_left, both))
        return both, at_left, at_right

    left_both, left_at_left, left_at_right = border(images[0:6])
    right_both, right_at_left, right_at_right = border(images[2:8])
    in_left = jnp.logical_and(has_left, jnp.logical_or(left_both, left_at_right))
    in_right = jnp.logical_and(has_right, jnp.logical_or(right_both, right_at_left))
    here = (left_both, in_left, in_left, True, True, in_right, in_right, right_both)
    names = []
    for place, present in enumerate(here):
        names.append(images[place] if present is True else jnp.where(present, images[place], -3 - place))
    for row in range(WINDOW):
        for column in range(WINDOW):
            level = jnp.where(names[row] == names[column], 0.0, -jnp.inf).astype(jnp.float32)
            bias[row : row + 1, column * TILE : (column + 1) * TILE] = jnp.full(
                (1, TILE), level, jnp.float32
            )
    from_left = [jnp.logical_and(images[w] == images[2], left_at_left) for w in (3, 4)]
    from_right = [jnp.logical_and(images[w] == images[5], right_at_right) for w in (3, 4)]
    mine = {}
    for w in (1, 2):
        mine[w] = jnp.logical_and(images[w] == images[3], left_at_right)
    for w in (5, 6):
        mine[w] = jnp.logical_and(images[w] == images[4], right_at_left)
    for index, w in enumerate((3, 4)):
        mine[w] = jnp.logical_not(jnp.logical_or(from_left[index], from_right[index]))
    squares[...] = jnp.zeros((8, 128), jnp.float32)

    pl.semaphore_wait(barrier, len(near))

    def loaded(head):
        for slot, source in enumerate((q_hbm, k_hbm, v_hbm, g_hbm)):
            load(source, slot, head).wait()

    for head in range(2):
        loaded(head)
        m_start(m_inputs, head)
    hops = max(line // 2, heads_axis // 2 + dps // (2 * cores) + cores - 1)
    for _ in range(max(hops - 1 - heads, 1)):
        give_tokens()
        take_tokens()

    def add_squares(value, flag):
        wide = value.astype(jnp.float32)
        wide = jnp.sum((wide * wide).reshape(TILE // 8, 8, HEAD_DIM), axis=0)
        squares[...] += jnp.where(flag, wide, 0.0)

    def compute(head):
        dk_acc[...] = jnp.zeros((HEAD_DIM, ROWS), jnp.float32)
        dv_acc[...] = jnp.zeros((HEAD_DIM, ROWS), jnp.float32)
        lanes = (((1,), (1,)), ((), ()))
        rows = (((0,), (0,)), ((), ()))
        wide = jnp.float32

        def block(index, carry):
            here = pl.ds(pl.multiple_of(index * BLOCK, BLOCK), BLOCK)
            query = win[head, 0, here, :]
            grad = win[head, 3, here, :]
            keys = win[head, 1]
            values = win[head, 2]
            scores = lax.dot_general(query, keys, lanes, preferred_element_type=wide) * scale
            pieces = []
            for half in range(BLOCK // TILE):
                row = bias[pl.ds(index * (BLOCK // TILE) + half, 1), :]
                pieces.append(scores[half * TILE : (half + 1) * TILE] + row)
            scores = jnp.concatenate(pieces, axis=0)
            raised = jnp.exp(scores - jnp.max(scores, axis=1, keepdims=True))
            weights = raised * (1.0 / jnp.sum(raised, axis=1, keepdims=True))
            weights = weights.astype(jnp.bfloat16)
            out = jnp.dot(weights, values, preferred_element_type=wide).astype(jnp.bfloat16)
            outs[head, 0, here, :] = out
            delta = jnp.sum(grad.astype(wide) * out.astype(wide), axis=1, keepdims=True)
            dweights = lax.dot_general(grad, values, lanes, preferred_element_type=wide)
            dscores = (weights.astype(wide) * (dweights - delta)).astype(jnp.bfloat16)
            dquery = jnp.dot(dscores, keys, preferred_element_type=wide) * scale
            outs[head, 1, here, :] = dquery.astype(jnp.bfloat16)
            dk_acc[...] += lax.dot_general(query, dscores, rows, preferred_element_type=wide)
            dv_acc[...] += lax.dot_general(grad, weights, rows, preferred_element_type=wide)
            return carry

        lax.fori_loop(0, ROWS // BLOCK, block, 0)
        for w in range(1, WINDOW - 1):
            dk = jnp.transpose(dk_acc[:, w * TILE : (w + 1) * TILE] * scale).astype(jnp.bfloat16)
            dv = jnp.transpose(dv_acc[:, w * TILE : (w + 1) * TILE]).astype(jnp.bfloat16)
            outs[head, 2, rows_of(w), :] = dk
            outs[head, 3, rows_of(w), :] = dv
            add_squares(outs[head, 1, rows_of(w), :], mine[w])
            add_squares(dk, mine[w])
            add_squares(dv, mine[w])

    out_refs = (o_ref, dq_ref, dk_ref, dv_ref)

    def assemble(head):
        column = pl.ds(pl.multiple_of(head * HEAD_DIM, HEAD_DIM), HEAD_DIM)
        for slot, out_ref in enumerate(out_refs):
            for index in range(OWN):
                value = outs[head, slot, rows_of(3 + index), :]
                other = got_m[0, head + LAG, slot, rows_of(index), :]
                value = jnp.where(from_left[index], other, value)
                other = got_m[1, head + LAG, slot, rows_of(index), :]
                value = jnp.where(from_right[index], other, value)
                out_ref[0, rows_of(index), column] = value

    def fill_stage(turn):
        for way, switch, back in ((0, right_at_left, 5), (1, left_at_right, 1)):
            for slot in range(4):
                stage[way, turn - LAG, slot] = jnp.where(
                    switch,
                    outs[turn - LAG, slot, rows_of(back, 2), :],
                    win[turn, slot, rows_of(3, 2), :],
                )

    def arrive(head):
        m_wait_recv(head)
        t_start(head)
        pair = jnp.zeros((OWN * TILE, HEAD_DIM), jnp.bfloat16)
        for slot in range(4):
            win[head, slot, rows_of(1, 2), :] = jnp.where(in_left, got_m[0, head, slot], pair)
            win[head, slot, rows_of(5, 2), :] = jnp.where(in_right, got_m[1, head, slot], pair)

    arrive(0)
    loaded(2)
    m_start(m_inputs, 2)

    def step(head, carry):
        @pl.when(head < heads - 2)
        def _():
            arrive(head + 1)

        give_tokens()
        t_wait_recv(head)
        blank = jnp.zeros((TILE, HEAD_DIM), jnp.bfloat16)
        for slot in range(4):
            win[head, slot, rows_of(0), :] = jnp.where(left_both, got_t[0, head, slot], blank)
            win[head, slot, rows_of(7), :] = jnp.where(right_both, got_t[1, head, slot], blank)
        compute(head)

        @pl.when(head == heads - 3)
        def _():
            arrive(heads - 1)

        @pl.when(head + LAG < heads)
        def _():
            loaded(head + LAG)
            fill_stage(head + LAG)
            m_start(m_either, head + LAG)

        @pl.when(jnp.logical_and(head + LAG >= heads, head < heads - 1))
        def _():
            m_start(m_results, head + LAG)

        take_tokens()

        @pl.when(jnp.logical_and(head >= 2, head < heads - 1))
        def _():
            assemble(head - 2)

        return carry

    lax.fori_loop(0, heads, step, 0)

    own_sum[...] = jnp.sum(squares[...], axis=0, keepdims=True)
    line_sums[pl.ds(me, 1)] = own_sum[...][None]

    def line_copy(step):
        return pltpu.make_async_remote_copy(
            src_ref=own_sum,
            dst_ref=line_sums.at[me],
            send_sem=line_send.at[step],
            recv_sem=line_recv.at[me],
            device_id={"seq": lax.rem(me + step, line)},
            device_id_type=MESH,
        )

    def line_arrival(step):
        peer = lax.rem(me + step, line)
        return pltpu.make_async_remote_copy(
            src_ref=own_sum,
            dst_ref=line_sums.at[peer],
            send_sem=line_send.at[step],
            recv_sem=line_recv.at[peer],
            device_id={"seq": peer},
            device_id_type=MESH,
        )

    def over(count, action):
        def body(step, carry):
            action(step)
            return carry

        lax.fori_loop(1, count, body, 0)

    over(line, lambda step: line_copy(step).start())

    m_start(m_results, heads - 1 + LAG)
    for head in range(heads - LAG, heads - 1):
        m_wait_recv(head + LAG)
        assemble(head)

    over(line, lambda step: line_arrival(step).wait_recv())
    place = my_dp * heads_axis + my_head
    line_total = jnp.sum(line_sums[...], axis=0)
    plane_sums[pl.ds(place, 1)] = line_total[None]

    def plane_copy(step, slot):
        peer_dp, peer_head = plane_peer(step)
        return pltpu.make_async_remote_copy(
            src_ref=plane_sums.at[place],
            dst_ref=plane_sums.at[slot],
            send_sem=plane_send.at[step],
            recv_sem=plane_recv.at[slot],
            device_id={"dp": peer_dp, "head": peer_head},
            device_id_type=MESH,
        )

    plane = dps * heads_axis
    over(plane, lambda step: plane_copy(step, place).start())

    m_wait_recv(heads - 1 + LAG)
    assemble(heads - 1)

    over(plane, lambda step: plane_copy(step, lax.rem(place + step, plane)).wait_recv())
    everything = jnp.sum(plane_sums[...], axis=0)
    everything = jnp.sum(everything, axis=1, keepdims=True)
    everything = jnp.sum(everything, axis=0, keepdims=True)
    rms_ref[0] = jnp.sqrt(everything * (1.0 / total))[0, 0]

    for turn in range(heads + LAG):
        m_wait_send(m_inputs if turn < LAG else m_either if turn < heads else m_results, turn)
    for head in range(heads):
        t_wait_send(head)
    over(line, lambda step: line_copy(step).wait_send())
    over(plane, lambda step: plane_copy(step, place).wait_send())


def flush(*refs):
    sources, targets, sems = refs[:4], refs[4:8], refs[8]
    copies = [
        pltpu.make_async_copy(sources[slot], targets[slot], sems.at[slot]) for slot in range(4)
    ]
    for copy in copies:
        copy.start()
    for copy in copies:
        copy.wait()


def solution(mesh):
    line, dps, heads_axis = mesh.shape["seq"], mesh.shape["dp"], mesh.shape["head"]

    def shards(queries, key_rows, value_rows, out_grad, tile_image):
        _, rows, features = queries.shape
        heads = features // HEAD_DIM
        total = 3.0 * rows * features * line * dps * heads_axis
        result = jax.ShapeDtypeStruct((1, rows, features), jnp.bfloat16)
        tile, pair = (4, TILE, HEAD_DIM), (4, OWN * TILE, HEAD_DIM)
        bf16, f32 = jnp.bfloat16, jnp.float32
        dma = pltpu.SemaphoreType.DMA
        vmem = pl.BlockSpec(memory_space=pltpu.VMEM)
        smem = pl.BlockSpec(memory_space=pltpu.SMEM)
        hbm = pl.BlockSpec(memory_space=pltpu.HBM)
        anywhere = pl.BlockSpec(memory_space=pl.ANY)
        outputs = pl.pallas_call(
            functools.partial(
                kernel, heads=heads, line=line, dps=dps, heads_axis=heads_axis, total=total
            ),
            out_shape=(result, result, result, result, jax.ShapeDtypeStruct((1,), f32)),
            in_specs=[smem, hbm, hbm, hbm, hbm],
            out_specs=(vmem, vmem, vmem, vmem, smem),
            scratch_shapes=[
                pltpu.VMEM((heads, 4, ROWS, HEAD_DIM), bf16),
                pltpu.VMEM((heads, 4, ROWS, HEAD_DIM), bf16),
                pltpu.VMEM((2, heads - LAG) + pair, bf16),
                pltpu.VMEM((2, heads + LAG) + pair, bf16),
                pltpu.VMEM((2, heads) + tile, bf16),
                pltpu.VMEM((WINDOW, ROWS), f32),
                pltpu.VMEM((HEAD_DIM, ROWS), f32),
                pltpu.VMEM((HEAD_DIM, ROWS), f32),
                pltpu.VMEM((8, 128), f32),
                pltpu.VMEM((1, 128), f32),
                pltpu.VMEM((line, 1, 128), f32),
                pltpu.VMEM((dps * heads_axis, 1, 128), f32),
                dma((heads, 4)),
                dma((2, heads + LAG)),
                dma((2, heads + LAG)),
                dma((2, heads)),
                dma((2, heads)),
                pltpu.SemaphoreType.REGULAR((7,)),
                dma((line,)),
                dma((line,)),
                dma((dps * heads_axis,)),
                dma((dps * heads_axis,)),
            ],
            compiler_params=pltpu.CompilerParams(
                collective_id=0, has_side_effects=True, vmem_limit_bytes=48 * 1024 * 1024
            ),
        )(*[pltpu.with_memory_space_constraint(x, pltpu.HBM) for x in (tile_image, queries, key_rows, value_rows, out_grad)])
        written = pl.pallas_call(
            flush,
            out_shape=(result, result, result, result),
            in_specs=[anywhere] * 4,
            out_specs=(hbm, hbm, hbm, hbm),
            scratch_shapes=[dma((4,))],
            compiler_params=pltpu.CompilerParams(vmem_limit_bytes=8 * 1024 * 1024),
        )(*outputs[:4])
        return tuple(written) + (outputs[4].reshape(()),)

    wide = P("dp", "seq", "head")
    return jax.shard_map(
        shards,
        mesh=mesh,
        in_specs=(wide, wide, wide, wide, P("dp", None)),
        out_specs=(wide, wide, wide, wide, P()),
        check_vma=False,
    )
```

time: 121 us -> 95.6 us (0.79)
  Pallas kernels: 110 us -> 93.1 us
  local copies, waits for them, and re-layouts: 7.61 us -> 0 us
    pallas_call x1, Pallas kernels: 110 us -> 91.9 us  [shards(): pl.pallas_call(functools.partial(kernel, heads=heads, line=line, dps=dps,...]
    unnamed x14 -> x0, local copies, waits for them, and re-layouts: 7.61 us -> none
where the time goes in v1:
time: 95.6 us; the launch traced here: 95.5 us
  Pallas kernels  93.1 us (97%)
  between operations  2.41 us (3%)
    pallas_call x1, Pallas kernels, shards(): pl.pallas_call(functools.partial(kernel, heads=heads, line=line, dps=dps,...  91.9 us

profile of v1, /device:TPU:1, one launch (start us, length us, event | category | flops | bytes accessed | tf_op | source)
XLA Modules:
  0.0 95.5 jit_solution(14256878778131439516)
XLA Ops:
  0.6 91.9 %shard_map.92 = (bf16[1,256,768]{2,1,0:T(8,128)(2,1)S(1)}, bf16[1,256,768]{2,1,0:T(8,128)(2,1)S(1)}, bf16[1,256,768]{2,1,0:T(8,128)(2,1)S(1)}, bf16[1,256,768]{2,1,0:T(8,128)(2,1)S(1)}, f32[1]{0:T(128)}) custom-call(s32[1,32]{1,0:T(1,128)} %tiles_ref.1, bf16[1,256,768]{2,1,0:T(8,128)(2,1)} %q_hbm.1, bf16[1,256,768]{2,1,0:T(8,128)(2,1)} %k_hbm.1, ...), custom_call_target="tpu_custom_call" | custom-call | tf_op jit(solution)/shard_map/pallas_call | solution.py:483
  92.5 1.2 %shard_map.93 = (bf16[1,256,768]{2,1,0:T(8,128)(2,1)}, bf16[1,256,768]{2,1,0:T(8,128)(2,1)}, bf16[1,256,768]{2,1,0:T(8,128)(2,1)}, bf16[1,256,768]{2,1,0:T(8,128)(2,1)}) custom-call(bf16[1,256,768]{2,1,0:T(8,128)(2,1)S(1)} %get-tuple-element.14.refs_0_, bf16[1,256,768]{2,1,0:T(8,128)(2,1)S(1)} %get-tuple-element.15.refs_1_, ...), custom_call_target="tpu_custom_call" | custom-call | tf_op jit(solution)/shard_map/pallas_call | solution.py:518

commit v2 on v1

--- a/solution.py
+++ b/solution.py
@@ -10,8 +10,10 @@
 HEAD_DIM = 128
 TILE = 128
 OWN = 2
-WINDOW = 8
-ROWS = WINDOW * TILE
+SIGHT = 8
+SLOTS = 6
+ROWS = SLOTS * TILE
+LOG2_E = 1.4426950408889634
 BLOCK = 256
 LAG = 3
 MESH = pl.DeviceIdType.MESH
@@ -74,7 +76,7 @@
     def load(source, slot, head):
         return pltpu.make_async_copy(
             source.at[0, :, pl.ds(head * HEAD_DIM, HEAD_DIM)],
-            win.at[head, slot, rows_of(3, 2), :],
+            win.at[head, slot, rows_of(2, 2), :],
             load_sem.at[head, slot],
         )
 
@@ -94,13 +96,13 @@
         )
 
     def m_inputs(turn, way):
-        return m_copy(turn, way, win.at[turn, :, rows_of(3, 2), :])
+        return m_copy(turn, way, win.at[turn, :, rows_of(2, 2), :])
 
     def m_either(turn, way):
         return m_copy(turn, way, stage.at[way, turn - LAG])
 
     def m_results(turn, way):
-        return m_copy(turn, way, outs.at[turn - LAG, :, rows_of(5 if way == 0 else 1, 2), :])
+        return m_copy(turn, way, outs.at[turn - LAG, :, rows_of(4 if way == 0 else 0, 2), :])
 
     def t_copy(head, way):
         return sent(
@@ -204,7 +206,7 @@
         pl.semaphore_signal(barrier, inc=1, device_id=peer, device_id_type=MESH)
 
     images = []
-    for place in range(WINDOW):
+    for place in range(SIGHT):
         tile = OWN * me - 3 + place
         image = tiles_ref[0, jnp.clip(tile, 0, tile_count - 1)]
         image = jnp.where(tile < 0, -1, image)
@@ -226,12 +228,16 @@
     right_both, right_at_left, right_at_right = border(images[2:8])
     in_left = jnp.logical_and(has_left, jnp.logical_or(left_both, left_at_right))
     in_right = jnp.logical_and(has_right, jnp.logical_or(right_both, right_at_left))
-    here = (left_both, in_left, in_left, True, True, in_right, in_right, right_both)
-    names = []
-    for place, present in enumerate(here):
-        names.append(images[place] if present is True else jnp.where(present, images[place], -3 - place))
-    for row in range(WINDOW):
-        for column in range(WINDOW):
+    names = [
+        jnp.where(right_both, images[7], jnp.where(in_left, images[1], -3)),
+        jnp.where(in_left, images[2], -4),
+        images[3],
+        images[4],
+        jnp.where(in_right, images[5], -5),
+        jnp.where(left_both, images[0], jnp.where(in_right, images[6], -6)),
+    ]
+    for row in range(SLOTS):
+        for column in range(SLOTS):
             level = jnp.where(names[row] == names[column], 0.0, -jnp.inf).astype(jnp.float32)
             bias[row : row + 1, column * TILE : (column + 1) * TILE] = jnp.full(
                 (1, TILE), level, jnp.float32
@@ -279,13 +285,14 @@
             grad = win[head, 3, here, :]
             keys = win[head, 1]
             values = win[head, 2]
-            scores = lax.dot_general(query, keys, lanes, preferred_element_type=wide) * scale
+            scores = lax.dot_general(query, keys, lanes, preferred_element_type=wide)
+            scores = scores * (scale * LOG2_E)
             pieces = []
             for half in range(BLOCK // TILE):
                 row = bias[pl.ds(index * (BLOCK // TILE) + half, 1), :]
                 pieces.append(scores[half * TILE : (half + 1) * TILE] + row)
             scores = jnp.concatenate(pieces, axis=0)
-            raised = jnp.exp(scores - jnp.max(scores, axis=1, keepdims=True))
+            raised = jnp.exp2(scores - jnp.max(scores, axis=1, keepdims=True))
             weights = raised * (1.0 / jnp.sum(raised, axis=1, keepdims=True))
             weights = weights.astype(jnp.bfloat16)
             out = jnp.dot(weights, values, preferred_element_type=wide).astype(jnp.bfloat16)
@@ -300,12 +307,13 @@
             return carry
 
         lax.fori_loop(0, ROWS // BLOCK, block, 0)
-        for w in range(1, WINDOW - 1):
-            dk = jnp.transpose(dk_acc[:, w * TILE : (w + 1) * TILE] * scale).astype(jnp.bfloat16)
-            dv = jnp.transpose(dv_acc[:, w * TILE : (w + 1) * TILE]).astype(jnp.bfloat16)
-            outs[head, 2, rows_of(w), :] = dk
-            outs[head, 3, rows_of(w), :] = dv
-            add_squares(outs[head, 1, rows_of(w), :], mine[w])
+        for w in range(1, SLOTS + 1):
+            slot = w - 1
+            dk = jnp.transpose(dk_acc[:, slot * TILE : (slot + 1) * TILE] * scale).astype(jnp.bfloat16)
+            dv = jnp.transpose(dv_acc[:, slot * TILE : (slot + 1) * TILE]).astype(jnp.bfloat16)
+            outs[head, 2, rows_of(slot), :] = dk
+            outs[head, 3, rows_of(slot), :] = dv
+            add_squares(outs[head, 1, rows_of(slot), :], mine[w])
             add_squares(dk, mine[w])
             add_squares(dv, mine[w])
 
@@ -315,7 +323,7 @@
         column = pl.ds(pl.multiple_of(head * HEAD_DIM, HEAD_DIM), HEAD_DIM)
         for slot, out_ref in enumerate(out_refs):
             for index in range(OWN):
-                value = outs[head, slot, rows_of(3 + index), :]
+                value = outs[head, slot, rows_of(2 + index), :]
                 other = got_m[0, head + LAG, slot, rows_of(index), :]
                 value = jnp.where(from_left[index], other, value)
                 other = got_m[1, head + LAG, slot, rows_of(index), :]
@@ -323,12 +331,12 @@
                 out_ref[0, rows_of(index), column] = value
 
     def fill_stage(turn):
-        for way, switch, back in ((0, right_at_left, 5), (1, left_at_right, 1)):
+        for way, switch, back in ((0, right_at_left, 4), (1, left_at_right, 0)):
             for slot in range(4):
                 stage[way, turn - LAG, slot] = jnp.where(
                     switch,
                     outs[turn - LAG, slot, rows_of(back, 2), :],
-                    win[turn, slot, rows_of(3, 2), :],
+                    win[turn, slot, rows_of(2, 2), :],
                 )
 
     def arrive(head):
@@ -336,8 +344,8 @@
         t_start(head)
         pair = jnp.zeros((OWN * TILE, HEAD_DIM), jnp.bfloat16)
         for slot in range(4):
-            win[head, slot, rows_of(1, 2), :] = jnp.where(in_left, got_m[0, head, slot], pair)
-            win[head, slot, rows_of(5, 2), :] = jnp.where(in_right, got_m[1, head, slot], pair)
+            win[head, slot, rows_of(0, 2), :] = jnp.where(in_left, got_m[0, head, slot], pair)
+            win[head, slot, rows_of(4, 2), :] = jnp.where(in_right, got_m[1, head, slot], pair)
 
     arrive(0)
     loaded(2)
@@ -350,10 +358,11 @@
 
         give_tokens()
         t_wait_recv(head)
-        blank = jnp.zeros((TILE, HEAD_DIM), jnp.bfloat16)
         for slot in range(4):
-            win[head, slot, rows_of(0), :] = jnp.where(left_both, got_t[0, head, slot], blank)
-            win[head, slot, rows_of(7), :] = jnp.where(right_both, got_t[1, head, slot], blank)
+            for switch, way, outer in ((right_both, 1, 0), (left_both, 0, SLOTS - 1)):
+                win[head, slot, rows_of(outer), :] = jnp.where(
+                    switch, got_t[way, head, slot], win[head, slot, rows_of(outer), :]
+                )
         compute(head)
 
         @pl.when(head == heads - 3)
@@ -366,7 +375,7 @@
             fill_stage(head + LAG)
             m_start(m_either, head + LAG)
 
-        @pl.when(jnp.logical_and(head + LAG >= heads, head < heads - 1))
+        @pl.when(jnp.logical_and(head + LAG >= heads, head < heads - 2))
         def _():
             m_start(m_results, head + LAG)
 
@@ -413,6 +422,7 @@
 
     over(line, lambda step: line_copy(step).start())
 
+    m_start(m_results, heads - 2 + LAG)
     m_start(m_results, heads - 1 + LAG)
     for head in range(heads - LAG, heads - 1):
         m_wait_recv(head + LAG)
@@ -493,7 +503,7 @@
                 pltpu.VMEM((2, heads - LAG) + pair, bf16),
                 pltpu.VMEM((2, heads + LAG) + pair, bf16),
                 pltpu.VMEM((2, heads) + tile, bf16),
-                pltpu.VMEM((WINDOW, ROWS), f32),
+                pltpu.VMEM((SLOTS, ROWS), f32),
                 pltpu.VMEM((HEAD_DIM, ROWS), f32),
                 pltpu.VMEM((HEAD_DIM, ROWS), f32),
                 pltpu.VMEM((8, 128), f32),

time: 95.6 us -> 92.4 us (0.967)
  Pallas kernels: 93.1 us -> 89.8 us
    pallas_call x1, Pallas kernels: 91.9 us -> 88.6 us  [shards(): pl.pallas_call(functools.partial(kernel, heads=heads, line=line, dps=dps,...]
where the time goes in v2:
time: 92.4 us; the launch traced here: 92.2 us
  Pallas kernels  89.8 us (97%)
  between operations  2.41 us (3%)
    pallas_call x1, Pallas kernels, shards(): pl.pallas_call(functools.partial(kernel, heads=heads, line=line, dps=dps,...  88.6 us

profile of v2, /device:TPU:1, one launch (start us, length us, event | category | flops | bytes accessed | tf_op | source)
XLA Modules:
  0.0 92.2 jit_solution(9801483846437783698)
XLA Ops:
  0.6 88.6 %shard_map.92 = (bf16[1,256,768]{2,1,0:T(8,128)(2,1)S(1)}, bf16[1,256,768]{2,1,0:T(8,128)(2,1)S(1)}, bf16[1,256,768]{2,1,0:T(8,128)(2,1)S(1)}, bf16[1,256,768]{2,1,0:T(8,128)(2,1)S(1)}, f32[1]{0:T(128)}) custom-call(s32[1,32]{1,0:T(1,128)} %tiles_ref.1, bf16[1,256,768]{2,1,0:T(8,128)(2,1)} %q_hbm.1, bf16[1,256,768]{2,1,0:T(8,128)(2,1)} %k_hbm.1, ...), custom_call_target="tpu_custom_call" | custom-call | tf_op jit(solution)/shard_map/pallas_call | solution.py:493
  89.3 1.2 %shard_map.93 = (bf16[1,256,768]{2,1,0:T(8,128)(2,1)}, bf16[1,256,768]{2,1,0:T(8,128)(2,1)}, bf16[1,256,768]{2,1,0:T(8,128)(2,1)}, bf16[1,256,768]{2,1,0:T(8,128)(2,1)}) custom-call(bf16[1,256,768]{2,1,0:T(8,128)(2,1)S(1)} %get-tuple-element.14.refs_0_, bf16[1,256,768]{2,1,0:T(8,128)(2,1)S(1)} %get-tuple-element.15.refs_1_, ...), custom_call_target="tpu_custom_call" | custom-call | tf_op jit(solution)/shard_map/pallas_call | solution.py:528

commit v3 on v2

--- a/solution.py
+++ b/solution.py
@@ -14,7 +14,7 @@
 SLOTS = 6
 ROWS = SLOTS * TILE
 LOG2_E = 1.4426950408889634
-BLOCK = 256
+BLOCK = 768
 LAG = 3
 MESH = pl.DeviceIdType.MESH
 
@@ -273,14 +273,12 @@
         squares[...] += jnp.where(flag, wide, 0.0)
 
     def compute(head):
-        dk_acc[...] = jnp.zeros((HEAD_DIM, ROWS), jnp.float32)
-        dv_acc[...] = jnp.zeros((HEAD_DIM, ROWS), jnp.float32)
         lanes = (((1,), (1,)), ((), ()))
         rows = (((0,), (0,)), ((), ()))
         wide = jnp.float32
 
         def block(index, carry):
-            here = pl.ds(pl.multiple_of(index * BLOCK, BLOCK), BLOCK)
+            here = pl.ds(0, BLOCK)
             query = win[head, 0, here, :]
             grad = win[head, 3, here, :]
             keys = win[head, 1]
@@ -302,11 +300,11 @@
             dscores = (weights.astype(wide) * (dweights - delta)).astype(jnp.bfloat16)
             dquery = jnp.dot(dscores, keys, preferred_element_type=wide) * scale
             outs[head, 1, here, :] = dquery.astype(jnp.bfloat16)
-            dk_acc[...] += lax.dot_general(query, dscores, rows, preferred_element_type=wide)
-            dv_acc[...] += lax.dot_general(grad, weights, rows, preferred_element_type=wide)
+            dk_acc[...] = lax.dot_general(query, dscores, rows, preferred_element_type=wide)
+            dv_acc[...] = lax.dot_general(grad, weights, rows, preferred_element_type=wide)
             return carry
 
-        lax.fori_loop(0, ROWS // BLOCK, block, 0)
+        block(0, 0)
         for w in range(1, SLOTS + 1):
             slot = w - 1
             dk = jnp.transpose(dk_acc[:, slot * TILE : (slot + 1) * TILE] * scale).astype(jnp.bfloat16)
@@ -414,11 +412,8 @@
         )
 
     def over(count, action):
-        def body(step, carry):
+        for step in range(1, count):
             action(step)
-            return carry
-
-        lax.fori_loop(1, count, body, 0)
 
     over(line, lambda step: line_copy(step).start())
 

time: 92.4 us -> 89.3 us (0.966)
  Pallas kernels: 89.8 us -> 86.7 us
    pallas_call x1, Pallas kernels: 88.6 us -> 85.5 us  [shards(): pl.pallas_call(functools.partial(kernel, heads=heads, line=line, dps=dps,...]
where the time goes in v3:
time: 89.3 us; the launch traced here: 89.1 us
  Pallas kernels  86.7 us (97%)
  between operations  2.41 us (3%)
    pallas_call x1, Pallas kernels, shards(): pl.pallas_call(functools.partial(kernel, heads=heads, line=line, dps=dps,...  85.5 us

profile of v3, /device:TPU:1, one launch (start us, length us, event | category | flops | bytes accessed | tf_op | source)
XLA Modules:
  0.0 89.1 jit_solution(13642135604487085588)
XLA Ops:
  0.6 85.5 %shard_map.92 = (bf16[1,256,768]{2,1,0:T(8,128)(2,1)S(1)}, bf16[1,256,768]{2,1,0:T(8,128)(2,1)S(1)}, bf16[1,256,768]{2,1,0:T(8,128)(2,1)S(1)}, bf16[1,256,768]{2,1,0:T(8,128)(2,1)S(1)}, f32[1]{0:T(128)}) custom-call(s32[1,32]{1,0:T(1,128)} %tiles_ref.1, bf16[1,256,768]{2,1,0:T(8,128)(2,1)} %q_hbm.1, bf16[1,256,768]{2,1,0:T(8,128)(2,1)} %k_hbm.1, ...), custom_call_target="tpu_custom_call" | custom-call | tf_op jit(solution)/shard_map/pallas_call | solution.py:488
  86.2 1.2 %shard_map.93 = (bf16[1,256,768]{2,1,0:T(8,128)(2,1)}, bf16[1,256,768]{2,1,0:T(8,128)(2,1)}, bf16[1,256,768]{2,1,0:T(8,128)(2,1)}, bf16[1,256,768]{2,1,0:T(8,128)(2,1)}) custom-call(bf16[1,256,768]{2,1,0:T(8,128)(2,1)S(1)} %get-tuple-element.14.refs_0_, bf16[1,256,768]{2,1,0:T(8,128)(2,1)S(1)} %get-tuple-element.15.refs_1_, ...), custom_call_target="tpu_custom_call" | custom-call | tf_op jit(solution)/shard_map/pallas_call | solution.py:523

commit v4 on v3

--- a/solution.py
+++ b/solution.py
@@ -373,10 +373,6 @@
             fill_stage(head + LAG)
             m_start(m_either, head + LAG)
 
-        @pl.when(jnp.logical_and(head + LAG >= heads, head < heads - 2))
-        def _():
-            m_start(m_results, head + LAG)
-
         take_tokens()
 
         @pl.when(jnp.logical_and(head >= 2, head < heads - 1))
@@ -417,6 +413,7 @@
 
     over(line, lambda step: line_copy(step).start())
 
+    m_start(m_results, heads - 3 + LAG)
     m_start(m_results, heads - 2 + LAG)
     m_start(m_results, heads - 1 + LAG)
     for head in range(heads - LAG, heads - 1):

time: 89.3 us -> 91.9 us (1.029)
  the two profiles are of different devices: /device:TPU:1 before, /device:TPU:33 now
where the time goes in v4:
time: 91.9 us; the launch traced here: 91.7 us
  Pallas kernels  89.3 us (97%)
  between operations  2.41 us (3%)
    pallas_call x1, Pallas kernels, shards(): pl.pallas_call(functools.partial(kernel, heads=heads, line=line, dps=dps,...  88.1 us

profile of v4, /device:TPU:33, one launch (start us, length us, event | category | flops | bytes accessed | tf_op | source)
XLA Modules:
  0.0 91.7 jit_solution(12102837689547211250)
XLA Ops:
  0.6 88.1 %shard_map.92 = (bf16[1,256,768]{2,1,0:T(8,128)(2,1)S(1)}, bf16[1,256,768]{2,1,0:T(8,128)(2,1)S(1)}, bf16[1,256,768]{2,1,0:T(8,128)(2,1)S(1)}, bf16[1,256,768]{2,1,0:T(8,128)(2,1)S(1)}, f32[1]{0:T(128)}) custom-call(s32[1,32]{1,0:T(1,128)} %tiles_ref.1, bf16[1,256,768]{2,1,0:T(8,128)(2,1)} %q_hbm.1, bf16[1,256,768]{2,1,0:T(8,128)(2,1)} %k_hbm.1, ...), custom_call_target="tpu_custom_call" | custom-call | tf_op jit(solution)/shard_map/pallas_call | solution.py:485
  88.8 1.2 %shard_map.93 = (bf16[1,256,768]{2,1,0:T(8,128)(2,1)}, bf16[1,256,768]{2,1,0:T(8,128)(2,1)}, bf16[1,256,768]{2,1,0:T(8,128)(2,1)}, bf16[1,256,768]{2,1,0:T(8,128)(2,1)}) custom-call(bf16[1,256,768]{2,1,0:T(8,128)(2,1)S(1)} %get-tuple-element.14.refs_0_, bf16[1,256,768]{2,1,0:T(8,128)(2,1)S(1)} %get-tuple-element.15.refs_1_, ...), custom_call_target="tpu_custom_call" | custom-call | tf_op jit(solution)/shard_map/pallas_call | solution.py:520
